TPU v7x, 32 devices: a whole 2x2x4 slice. The times are simulated.
32 devices in a mesh: sa: 4 (over y, core), sb: 8 (over z, x).
Axes of the slice: x: 2, y: 2, z: 4, core: 2. Of those that a mesh axis runs over, the one named last changes fastest.
Arguments:
- queries: bfloat16 [1024, 1024], P(('sa', 'sb')), may hold values from -6 to 6
- out_grad: bfloat16 [1024, 1024], P(('sa', 'sb')), may hold values from -6144 to 6144
- forward_out: bfloat16 [1024, 1024], P(('sa', 'sb')), may hold values from -3 to 3
- lse_shift: float32 [1024, 8], P(('sa', 'sb')), may hold values from 0.2 to 1
- key_rows: bfloat16 [32768, 256], P(('sa', 'sb')), may hold values from -7 to 7
- value_rows: bfloat16 [32768, 256], P(('sa', 'sb')), may hold values from -6 to 6
Outputs:
- query_grad: float32 [1024, 1024], P(('sa', 'sb'))
- key_grad: bfloat16 [32768, 256], P(('sa', 'sb'))
- value_grad: bfloat16 [32768, 256], P(('sa', 'sb'))
All inputs are finite; a program needn't handle non-finite values.
Results may differ from a plain program's by a relative error of at most 0.0097.
Values may be sent and summed in bfloat16 or wider, within the bound.
A program may use at most 64 MiB of HBM per device.

v0:
```python
import math
import jax
import jax.numpy as jnp
from jax import lax
from jax.sharding import PartitionSpec as P

QH = 8
KVH = 2
HEAD_DIM = 128


def head_delta(grad_part, output_part):
    product = grad_part.astype(jnp.float32) * output_part.astype(jnp.float32)
    return jnp.sum(product.reshape(product.shape[0], QH, HEAD_DIM), axis=-1)


def local(queries, out_grad, forward_out, lse_shift, key_rows, value_rows):
    per_group = QH // KVH
    score_scale = 1.0 / math.sqrt(HEAD_DIM)
    devices = lax.axis_size("sa") * lax.axis_size("sb")
    local_keys = key_rows.shape[0]
    total_keys = local_keys * devices
    key_total = lax.psum(jnp.sum(key_rows.astype(jnp.float32), axis=0), ("sa", "sb"))
    smoothed = (key_rows.astype(jnp.float32) - key_total / total_keys).astype(jnp.bfloat16)
    query_all, grad_all, output_all = (
        lax.all_gather(queries, ("sa", "sb"), axis=0, tiled=True),
        lax.all_gather(out_grad, ("sa", "sb"), axis=0, tiled=True),
        lax.all_gather(forward_out, ("sa", "sb"), axis=0, tiled=True),
    )
    shift_all = lax.all_gather(lse_shift, ("sa", "sb"), axis=0, tiled=True)
    delta_all = head_delta(grad_all, output_all)
    offset_all = shift_all + math.log(total_keys)

    def one_head(head):
        shared = head // per_group
        head_queries = lax.dynamic_slice_in_dim(query_all, head * HEAD_DIM, HEAD_DIM, 1)
        head_grads = lax.dynamic_slice_in_dim(grad_all, head * HEAD_DIM, HEAD_DIM, 1)
        head_keys = lax.dynamic_slice_in_dim(smoothed, shared * HEAD_DIM, HEAD_DIM, 1)
        head_values = lax.dynamic_slice_in_dim(value_rows, shared * HEAD_DIM, HEAD_DIM, 1)
        head_offset = lax.dynamic_slice_in_dim(offset_all, head, 1, 1)
        head_deltas = lax.dynamic_slice_in_dim(delta_all, head, 1, 1)
        scores = (
            jnp.einsum("qd,kd->qk", head_queries, head_keys, preferred_element_type=jnp.float32)
            * score_scale
        )
        prob = jnp.exp(scores - head_offset)
        prob_low = prob.astype(jnp.bfloat16)
        value_part = jnp.einsum(
            "qk,qd->kd", prob_low, head_grads, preferred_element_type=jnp.float32
        )
        dprob = jnp.einsum("qd,kd->qk", head_grads, head_values, preferred_element_type=jnp.float32)
        dscore = (prob * (dprob - head_deltas)).astype(jnp.bfloat16)
        key_part = (
            jnp.einsum("qk,qd->kd", dscore, head_queries, preferred_element_type=jnp.float32)
            * score_scale
        )
        query_part = (
            jnp.einsum("qk,kd->qd", dscore, head_keys, preferred_element_type=jnp.float32)
            * score_scale
        )
        return (query_part, key_part, value_part)

    query_heads, key_heads, value_heads = lax.map(one_head, jnp.arange(QH, dtype=jnp.int32))
    key_sum = key_heads.reshape(KVH, per_group, local_keys, HEAD_DIM).sum(axis=1)
    value_sum = value_heads.reshape(KVH, per_group, local_keys, HEAD_DIM).sum(axis=1)
    key_grad = key_sum.transpose(1, 0, 2).reshape(local_keys, KVH * HEAD_DIM).astype(jnp.bfloat16)
    value_grad = (
        value_sum.transpose(1, 0, 2).reshape(local_keys, KVH * HEAD_DIM).astype(jnp.bfloat16)
    )
    halfway = lax.psum_scatter(
        query_heads.astype(jnp.bfloat16), "sa", scatter_dimension=1, tiled=True
    )
    owned = lax.psum_scatter(halfway, "sb", scatter_dimension=1, tiled=True).astype(jnp.float32)
    query_grad = owned.transpose(1, 0, 2).reshape(owned.shape[1], QH * HEAD_DIM)
    return (query_grad, key_grad, value_grad)


def solution(mesh):
    in_specs = (
        P(("sa", "sb"), None),
        P(("sa", "sb"), None),
        P(("sa", "sb"), None),
        P(("sa", "sb"), None),
        P(("sa", "sb"), None),
        P(("sa", "sb"), None),
    )
    out_specs = (P(("sa", "sb"), None), P(("sa", "sb"), None), P(("sa", "sb"), None))
    return jax.shard_map(local, mesh=mesh, in_specs=in_specs, out_specs=out_specs, check_vma=False)
```

profile of v0, /device:TPU:0, one launch (start us, length us, event | category | flops | bytes accessed | tf_op | source)
XLA Modules:
  0.0 444.5 jit_solution(709339691636741124)
XLA Ops:
  9.5 70.8 %all-gather = f32[32,32,8]{1,2,0:T(8,128)S(1)} all-gather(f32[1,32,8]{1,2,0:T(8,128)} %bitcast.65), channel_id=1, replica_groups=mesh['sa'=4,'sb'=8] {'sa','sb'}, dimensions={0}, use_global_device_ids=true | all-gather | bytes 33792 | tf_op jit(solution)/shard_map/all_gather | solution.py:30
  81.6 37.2 %psum.7 = f32[256]{0:T(256)S(1)} all-reduce(f32[256]{0:T(256)S(1)} %convert_reduce_fusion), channel_id=1, replica_groups=mesh['sa'=4,'sb'=8] {'sa','sb'}, use_global_device_ids=true, to_apply=%region_1.0 | all-reduce | flops 256 | bytes 2048 | tf_op jit(solution)/shard_map/psum | solution.py:23
  120.0 9.0 %all-gather.9.cloned.1.call-done = bf16[1024,1024]{1,0:T(8,128)(2,1)} async-done(((bf16[32,1024]{1,0:T(8,128)(2,1)}), bf16[1024,1024]{1,0:T(8,128)(2,1)}) %all-gather.9.cloned.1.call-update) | async-done | bytes 2097168 | tf_op jit(solution)/shard_map/all_gather | solution.py:28
  128.9 3.1 multiply_bitcast_fusion
  132.1 3.0 copy.21
  135.0 3.4 reduce_sum.37
  138.6 48.5 %all-gather.5.cloned.1.call-done = bf16[1024,1024]{1,0:T(8,128)(2,1)} async-done(((bf16[32,1024]{1,0:T(8,128)(2,1)}), bf16[1024,1024]{1,0:T(8,128)(2,1)}) %all-gather.5.cloned.1.call-update) | async-done | bytes 2097168 | tf_op jit(solution)/shard_map/all_gather | solution.py:26
  187.2 152.8 %while.16 = (s32[]{:T(128)}, bf16[8,1024,128]{2,1,0:T(8,128)(2,1)}, f32[8,1024,128]{2,1,0:T(8,128)}, f32[8,1024,128]{2,1,0:T(8,128)}, s32[8]{0:T(128)S(1)}, /*in...) while((s32[]{:T(128)}, bf16[8,1024,128]{2,1,0:T(8,128)(2,1)}, ...), condition=%wide.region_4.5_spmd, body=%wide.region_3.4_spmd.sunk | while | flops 1350828032 | bytes 39090184 | solution.py:63
  191.0 3.6 fusion.56
  196.0 3.5 multiply_convert_fusion.2
  199.4 2.5 fusion.58
  201.9 2.9 fusion.59
  210.1 3.6 fusion.56
  215.0 3.5 multiply_convert_fusion.2
  218.5 2.5 fusion.58
  221.0 2.9 fusion.59
  229.2 3.6 fusion.56
  234.1 3.5 multiply_convert_fusion.2
  237.6 2.5 fusion.58
  240.1 2.9 fusion.59
  248.3 3.6 fusion.56
  253.2 3.5 multiply_convert_fusion.2
  256.7 2.5 fusion.58
  259.2 2.9 fusion.59
  267.4 3.6 fusion.56
  272.4 3.5 multiply_convert_fusion.2
  275.8 2.5 fusion.58
  278.3 2.9 fusion.59
  281.2 1.4 fusion.57
  286.5 3.6 fusion.56
  291.5 3.5 multiply_convert_fusion.2
  294.9 2.5 fusion.58
  297.5 2.9 fusion.59
  300.4 1.4 fusion.57
  305.6 3.6 fusion.56
  310.6 3.5 multiply_convert_fusion.2
  314.1 2.5 fusion.58
  316.6 2.9 fusion.59
  319.4 1.4 fusion.57
  324.7 3.6 fusion.56
  329.7 3.5 multiply_convert_fusion.2
  333.2 2.5 fusion.58
  335.7 2.9 fusion.59
  338.6 1.4 fusion.57
  340.1 30.1 %reduce-scatter.3.cloned.1.call-done = bf16[8,256,128]{2,1,0:T(8,128)(2,1)} async-done(((bf16[8,1024,128]{2,1,0:T(8,128)(2,1)}), bf16[8,256,128]{2,1,0:T(8,128)(2,1)}) %reduce-scatter.3.cloned.1.call-update) | async-done | bytes 524304 | tf_op jit(solution)/shard_map/reduce_scatter | solution.py:70
  370.2 4.3 bitcast_reduce_fusion
  377.0 59.4 %reduce-scatter.5.cloned.1.call-done = bf16[8,32,128]{2,1,0:T(8,128)(2,1)} async-done(((bf16[8,256,128]{2,1,0:T(8,128)(2,1)}), bf16[8,32,128]{2,1,0:T(8,128)(2,1)}) %reduce-scatter.5.cloned.1.call-update) | async-done | bytes 65552 | tf_op jit(solution)/shard_map/reduce_scatter | solution.py:73
  436.4 1.5 copy_bitcast_fusion
  (64 shorter events, 17.8 us)
Async XLA Ops:
  7.2 112.8 %all-gather.7.cloned.1.call-start = ((), (), s32[]{:S(2)}) async-start(), calls=%async_computation.3 | async-start | bytes 2162688 | tf_op jit(solution)/shard_map/all_gather | solution.py:27
  7.9 121.0 %all-gather.9.cloned.1.call-start = ((), (), s32[]{:S(2)}) async-start(), calls=%async_computation.4 | async-start | bytes 2162688 | tf_op jit(solution)/shard_map/all_gather | solution.py:28
  8.6 178.5 %all-gather.5.cloned.1.call-start = ((), (), s32[]{:S(2)}) async-start(), calls=%async_computation.2 | async-start | bytes 2162688 | tf_op jit(solution)/shard_map/all_gather | solution.py:26
  9.4 360.8 %reduce-scatter.3.cloned.1.call-start = ((), (), s32[]{:S(2)}) async-start(), calls=%async_computation.5 | async-start | bytes 2621440 | tf_op jit(solution)/shard_map/reduce_scatter | solution.py:70
  135.0 52.1 %copy-start.1 = (bf16[1024,256]{1,0:T(8,128)(2,1)S(1)}, bf16[1024,256]{1,0:T(8,128)(2,1)}, u32[]{:S(2)}) copy-start(bf16[1024,256]{1,0:T(8,128)(2,1)} %param.13) | copy-start | bytes 1572868
  196.0 6.0 %copy-start = (f32[1024,1024]{1,0:T(8,128)S(1)}, f32[1024,1024]{1,0:T(8,128)}, u32[]{:S(2)}) copy-start(f32[1024,1024]{1,0:T(8,128)} %fusion.56) | copy-start | bytes 12582916 | tf_op jit(solution)/shard_map/while
  215.0 6.0 %copy-start = (f32[1024,1024]{1,0:T(8,128)S(1)}, f32[1024,1024]{1,0:T(8,128)}, u32[]{:S(2)}) copy-start(f32[1024,1024]{1,0:T(8,128)} %fusion.56) | copy-start | bytes 12582916 | tf_op jit(solution)/shard_map/while
  234.1 6.0 %copy-start = (f32[1024,1024]{1,0:T(8,128)S(1)}, f32[1024,1024]{1,0:T(8,128)}, u32[]{:S(2)}) copy-start(f32[1024,1024]{1,0:T(8,128)} %fusion.56) | copy-start | bytes 12582916 | tf_op jit(solution)/shard_map/while
  253.2 6.0 %copy-start = (f32[1024,1024]{1,0:T(8,128)S(1)}, f32[1024,1024]{1,0:T(8,128)}, u32[]{:S(2)}) copy-start(f32[1024,1024]{1,0:T(8,128)} %fusion.56) | copy-start | bytes 12582916 | tf_op jit(solution)/shard_map/while
  272.4 6.0 %copy-start = (f32[1024,1024]{1,0:T(8,128)S(1)}, f32[1024,1024]{1,0:T(8,128)}, u32[]{:S(2)}) copy-start(f32[1024,1024]{1,0:T(8,128)} %fusion.56) | copy-start | bytes 12582916 | tf_op jit(solution)/shard_map/while
  291.5 6.0 %copy-start = (f32[1024,1024]{1,0:T(8,128)S(1)}, f32[1024,1024]{1,0:T(8,128)}, u32[]{:S(2)}) copy-start(f32[1024,1024]{1,0:T(8,128)} %fusion.56) | copy-start | bytes 12582916 | tf_op jit(solution)/shard_map/while
  310.6 6.0 %copy-start = (f32[1024,1024]{1,0:T(8,128)S(1)}, f32[1024,1024]{1,0:T(8,128)}, u32[]{:S(2)}) copy-start(f32[1024,1024]{1,0:T(8,128)} %fusion.56) | copy-start | bytes 12582916 | tf_op jit(solution)/shard_map/while
  329.7 6.0 %copy-start = (f32[1024,1024]{1,0:T(8,128)S(1)}, f32[1024,1024]{1,0:T(8,128)}, u32[]{:S(2)}) copy-start(f32[1024,1024]{1,0:T(8,128)} %fusion.56) | copy-start | bytes 12582916 | tf_op jit(solution)/shard_map/while
  340.0 96.4 %reduce-scatter.5.cloned.1.call-start = ((), (), s32[]{:S(2)}) async-start(), calls=%async_computation.6 | async-start | bytes 589824 | tf_op jit(solution)/shard_map/reduce_scatter | solution.py:73
Sparse Core Ops, SparseCore 0:
  11.0 59.4 all-gather.6
  73.4 55.4 all-gather.8
  131.9 55.1 all-gather.4
  340.1 30.0 reduce-scatter.2
  373.4 63.0 reduce-scatter.4
where the time goes:
time: 446 us; the launch traced here: 444 us
  waiting for transfers between devices  149 us (33%)
  matrix products  111 us (25%)
  blocking collectives  108 us (24%)
  loops' own time  36.7 us (8%)
  other arithmetic  14.7 us (3%)
  between operations  13.9 us (3%)
  local copies, waits for them, and re-layouts  10.5 us (2%)
    all_gather x1, blocking collectives, local(): shift_all = lax.all_gather(lse_shift, ('sa', 'sb'), axis=0, tiled=True)  70.8 us
    reduce_scatter x1, waiting for transfers between devices, local(): lax.psum_scatter(halfway, 'sb', scatter_dimension=1, tiled=True)  59.4 us
    all_gather x1, waiting for transfers between devices, local(): lax.all_gather(queries, ('sa', 'sb'), axis=0, tiled=True)  48.5 us
    psum x1, blocking collectives, local(): lax.psum(jnp.sum(key_rows.astype(jnp.float32), axis=0), ('sa', 'sb'))  37.2 us
    another operation x1, loops' own time, local(): lax.map(one_head, jnp.arange(QH, dtype=jnp.int32))  36.7 us
    reduce_scatter x1, waiting for transfers between devices, local(): lax.psum_scatter(query_heads.astype(jnp.bfloat16), 'sa', scatter_dimensio...  30.1 us
    dot_general x8, matrix products, one_head(): jnp.einsum('qd,kd->qk', head_queries, head_keys, preferred_element_type=j...  29.1 us
    dot_general x8, matrix products, one_head(): jnp.einsum('qd,kd->qk', head_grads, head_values, preferred_element_type=j...  27.7 us
  transfers between devices with their start and end apart: 5, of which 4 were waited for; matrix products, arithmetic and copies ran while one was open for 4% of the time, Pallas kernels for 0%

commit v1 on v0

--- a/solution.py
+++ b/solution.py
@@ -20,7 +20,9 @@
     devices = lax.axis_size("sa") * lax.axis_size("sb")
     local_keys = key_rows.shape[0]
     total_keys = local_keys * devices
-    key_total = lax.psum(jnp.sum(key_rows.astype(jnp.float32), axis=0), ("sa", "sb"))
+    own = jnp.sum(key_rows.astype(jnp.float32), axis=0)
+    pieces = lax.all_gather(own, ("sa", "sb"))
+    key_total = jnp.sum(pieces, axis=0)
     smoothed = (key_rows.astype(jnp.float32) - key_total / total_keys).astype(jnp.bfloat16)
     query_all, grad_all, output_all = (
         lax.all_gather(queries, ("sa", "sb"), axis=0, tiled=True),

time: 446 us -> 446 us (level)
  blocking collectives: 108 us -> 134 us
  waiting for transfers between devices: 149 us -> 123 us
    all_gather x0 -> x1, blocking collectives: none -> 63.6 us  [local(): pieces = lax.all_gather(own, ('sa', 'sb'))]
    psum x1 -> x0, blocking collectives: 37.2 us -> none  [local(): lax.psum(jnp.sum(key_rows.astype(jnp.float32), axis=0), ('sa', 'sb'))]
    all_gather x1, waiting for transfers between devices: 48.5 us -> 30.8 us  [local(): lax.all_gather(queries, ('sa', 'sb'), axis=0, tiled=True)]
    all_gather x1, waiting for transfers between devices: 8.96 us -> 0.02 us  [local(): lax.all_gather(forward_out, ('sa', 'sb'), axis=0, tiled=True)]
  transfers between devices with their start and end apart: 5 -> 5, of which waited for: 4 -> 3; matrix products, arithmetic and copies ran while one was open for 4% -> 4% of each run, Pallas kernels for 0% -> 0%
where the time goes in v1:
time: 446 us; the launch traced here: 444 us
  blocking collectives  134 us (30%)
  waiting for transfers between devices  123 us (28%)
  matrix products  111 us (25%)
  loops' own time  36.7 us (8%)
  other arithmetic  14.8 us (3%)
  between operations  13.9 us (3%)
  local copies, waits for them, and re-layouts  10.5 us (2%)
    all_gather x1, blocking collectives, local(): shift_all = lax.all_gather(lse_shift, ('sa', 'sb'), axis=0, tiled=True)  70.8 us
    all_gather x1, blocking collectives, local(): pieces = lax.all_gather(own, ('sa', 'sb'))  63.6 us
    reduce_scatter x1, waiting for transfers between devices, local(): lax.psum_scatter(halfway, 'sb', scatter_dimension=1, tiled=True)  59.4 us
    another operation x1, loops' own time, local(): lax.map(one_head, jnp.arange(QH, dtype=jnp.int32))  36.7 us
    all_gather x1, waiting for transfers between devices, local(): lax.all_gather(queries, ('sa', 'sb'), axis=0, tiled=True)  30.8 us
    reduce_scatter x1, waiting for transfers between devices, local(): lax.psum_scatter(query_heads.astype(jnp.bfloat16), 'sa', scatter_dimensio...  30.1 us
    dot_general x8, matrix products, one_head(): jnp.einsum('qd,kd->qk', head_queries, head_keys, preferred_element_type=j...  29.1 us
    dot_general x8, matrix products, one_head(): jnp.einsum('qd,kd->qk', head_grads, head_values, preferred_element_type=j...  27.7 us
  transfers between devices with their start and end apart: 5, of which 3 were waited for; matrix products, arithmetic and copies ran while one was open for 4% of the time, Pallas kernels for 0%

profile of v1, /device:TPU:0, one launch (start us, length us, event | category | flops | bytes accessed | tf_op | source)
XLA Modules:
  0.0 444.3 jit_solution(3396659285432956975)
XLA Ops:
  9.5 70.8 %all-gather.2 = f32[32,32,8]{1,2,0:T(8,128)S(1)} all-gather(f32[1,32,8]{1,2,0:T(8,128)} %bitcast.67), channel_id=1, replica_groups=mesh['sa'=4,'sb'=8] {'sa','sb'}, dimensions={0}, use_global_device_ids=true | all-gather | bytes 33792 | tf_op jit(solution)/shard_map/all_gather | solution.py:32
  81.6 63.6 %all-gather.1 = f32[32,1,256]{2,1,0:T(1,128)S(1)} all-gather(f32[1,1,256]{2,1,0:T(1,128)S(1)} %bitcast.66), channel_id=2, replica_groups=mesh['sa'=4,'sb'=8] {'sa','sb'}, dimensions={0}, use_global_device_ids=true | all-gather | bytes 33792 | tf_op jit(solution)/shard_map/all_gather | solution.py:24
  146.5 3.1 multiply_bitcast_fusion
  149.6 3.0 copy.21
  152.6 3.4 reduce_sum.47
  156.2 30.8 %all-gather.7.cloned.1.call-done = bf16[1024,1024]{1,0:T(8,128)(2,1)} async-done(((bf16[32,1024]{1,0:T(8,128)(2,1)}), bf16[1024,1024]{1,0:T(8,128)(2,1)}) %all-gather.7.cloned.1.call-update) | async-done | bytes 2097168 | tf_op jit(solution)/shard_map/all_gather | solution.py:28
  187.0 152.8 %while.16 = (s32[]{:T(128)}, bf16[8,1024,128]{2,1,0:T(8,128)(2,1)}, f32[8,1024,128]{2,1,0:T(8,128)}, f32[8,1024,128]{2,1,0:T(8,128)}, s32[8]{0:T(128)S(1)}, /*in...) while((s32[]{:T(128)}, bf16[8,1024,128]{2,1,0:T(8,128)(2,1)}, ...), condition=%wide.region_4.5_spmd, body=%wide.region_3.4_spmd.sunk | while | flops 1350828032 | bytes 39090184 | solution.py:65
  190.8 3.6 fusion.56
  195.8 3.5 multiply_convert_fusion.2
  199.3 2.5 fusion.58
  201.8 2.9 fusion.59
  209.9 3.6 fusion.56
  214.8 3.5 multiply_convert_fusion.2
  218.3 2.5 fusion.58
  220.8 2.9 fusion.59
  229.0 3.6 fusion.56
  233.9 3.5 multiply_convert_fusion.2
  237.4 2.5 fusion.58
  239.9 2.9 fusion.59
  248.1 3.6 fusion.56
  253.1 3.5 multiply_convert_fusion.2
  256.5 2.5 fusion.58
  259.1 2.9 fusion.59
  261.9 1.4 fusion.57
  267.2 3.6 fusion.56
  272.2 3.5 multiply_convert_fusion.2
  275.6 2.5 fusion.58
  278.1 2.9 fusion.59
  281.0 1.4 fusion.57
  286.3 3.6 fusion.56
  291.3 3.5 multiply_convert_fusion.2
  294.8 2.5 fusion.58
  297.3 2.9 fusion.59
  300.2 1.4 fusion.57
  305.5 3.6 fusion.56
  310.4 3.5 multiply_convert_fusion.2
  313.9 2.5 fusion.58
  316.4 2.9 fusion.59
  319.2 1.4 fusion.57
  324.5 3.6 fusion.56
  329.5 3.5 multiply_convert_fusion.2
  333.0 2.5 fusion.58
  335.5 2.9 fusion.59
  338.4 1.4 fusion.57
  339.9 30.1 %reduce-scatter.3.cloned.1.call-done = bf16[8,256,128]{2,1,0:T(8,128)(2,1)} async-done(((bf16[8,1024,128]{2,1,0:T(8,128)(2,1)}), bf16[8,256,128]{2,1,0:T(8,128)(2,1)}) %reduce-scatter.3.cloned.1.call-update) | async-done | bytes 524304 | tf_op jit(solution)/shard_map/reduce_scatter | solution.py:72
  370.0 4.3 bitcast_reduce_fusion
  376.8 59.4 %reduce-scatter.5.cloned.1.call-done = bf16[8,32,128]{2,1,0:T(8,128)(2,1)} async-done(((bf16[8,256,128]{2,1,0:T(8,128)(2,1)}), bf16[8,32,128]{2,1,0:T(8,128)(2,1)}) %reduce-scatter.5.cloned.1.call-update) | async-done | bytes 65552 | tf_op jit(solution)/shard_map/reduce_scatter | solution.py:75
  436.2 1.5 copy_bitcast_fusion
  (65 shorter events, 16.5 us)
Async XLA Ops:
  7.2 139.3 %all-gather.9.cloned.1.call-start = ((), (), s32[]{:S(2)}) async-start(), calls=%async_computation.3 | async-start | bytes 2162688 | tf_op jit(solution)/shard_map/all_gather | solution.py:29
  7.9 138.5 %all-gather.11.cloned.1.call-start = ((), (), s32[]{:S(2)}) async-start(), calls=%async_computation.4 | async-start | bytes 2162688 | tf_op jit(solution)/shard_map/all_gather | solution.py:30
  8.6 178.3 %all-gather.7.cloned.1.call-start = ((), (), s32[]{:S(2)}) async-start(), calls=%async_computation.2 | async-start | bytes 2162688 | tf_op jit(solution)/shard_map/all_gather | solution.py:28
  9.4 360.6 %reduce-scatter.3.cloned.1.call-start = ((), (), s32[]{:S(2)}) async-start(), calls=%async_computation.5 | async-start | bytes 2621440 | tf_op jit(solution)/shard_map/reduce_scatter | solution.py:72
  152.6 34.4 %copy-start.1 = (bf16[1024,256]{1,0:T(8,128)(2,1)S(1)}, bf16[1024,256]{1,0:T(8,128)(2,1)}, u32[]{:S(2)}) copy-start(bf16[1024,256]{1,0:T(8,128)(2,1)} %param.13) | copy-start | bytes 1572868
  195.8 6.0 %copy-start = (f32[1024,1024]{1,0:T(8,128)S(1)}, f32[1024,1024]{1,0:T(8,128)}, u32[]{:S(2)}) copy-start(f32[1024,1024]{1,0:T(8,128)} %fusion.56) | copy-start | bytes 12582916 | tf_op jit(solution)/shard_map/while
  214.8 6.0 %copy-start = (f32[1024,1024]{1,0:T(8,128)S(1)}, f32[1024,1024]{1,0:T(8,128)}, u32[]{:S(2)}) copy-start(f32[1024,1024]{1,0:T(8,128)} %fusion.56) | copy-start | bytes 12582916 | tf_op jit(solution)/shard_map/while
  233.9 6.0 %copy-start = (f32[1024,1024]{1,0:T(8,128)S(1)}, f32[1024,1024]{1,0:T(8,128)}, u32[]{:S(2)}) copy-start(f32[1024,1024]{1,0:T(8,128)} %fusion.56) | copy-start | bytes 12582916 | tf_op jit(solution)/shard_map/while
  253.0 6.0 %copy-start = (f32[1024,1024]{1,0:T(8,128)S(1)}, f32[1024,1024]{1,0:T(8,128)}, u32[]{:S(2)}) copy-start(f32[1024,1024]{1,0:T(8,128)} %fusion.56) | copy-start | bytes 12582916 | tf_op jit(solution)/shard_map/while
  272.2 6.0 %copy-start = (f32[1024,1024]{1,0:T(8,128)S(1)}, f32[1024,1024]{1,0:T(8,128)}, u32[]{:S(2)}) copy-start(f32[1024,1024]{1,0:T(8,128)} %fusion.56) | copy-start | bytes 12582916 | tf_op jit(solution)/shard_map/while
  291.3 6.0 %copy-start = (f32[1024,1024]{1,0:T(8,128)S(1)}, f32[1024,1024]{1,0:T(8,128)}, u32[]{:S(2)}) copy-start(f32[1024,1024]{1,0:T(8,128)} %fusion.56) | copy-start | bytes 12582916 | tf_op jit(solution)/shard_map/while
  310.4 6.0 %copy-start = (f32[1024,1024]{1,0:T(8,128)S(1)}, f32[1024,1024]{1,0:T(8,128)}, u32[]{:S(2)}) copy-start(f32[1024,1024]{1,0:T(8,128)} %fusion.56) | copy-start | bytes 12582916 | tf_op jit(solution)/shard_map/while
  329.5 6.0 %copy-start = (f32[1024,1024]{1,0:T(8,128)S(1)}, f32[1024,1024]{1,0:T(8,128)}, u32[]{:S(2)}) copy-start(f32[1024,1024]{1,0:T(8,128)} %fusion.56) | copy-start | bytes 12582916 | tf_op jit(solution)/shard_map/while
  339.8 96.4 %reduce-scatter.5.cloned.1.call-start = ((), (), s32[]{:S(2)}) async-start(), calls=%async_computation.6 | async-start | bytes 589824 | tf_op jit(solution)/shard_map/reduce_scatter | solution.py:75
Sparse Core Ops, SparseCore 0:
  11.0 59.4 all-gather.8
  73.4 55.2 all-gather.10
  131.7 55.2 all-gather.6
  339.9 30.0 reduce-scatter.2
  373.2 63.0 reduce-scatter.4
